TPU v7x, 256 devices: a whole 4x4x8 slice. The times are simulated.
256 devices in a mesh: dp: 16 (over y, x), expert: 8 (over z), tensor: 2 (over core).
Axes of the slice: x: 4, y: 4, z: 8, core: 2. Of those that a mesh axis runs over, the one named last changes fastest.
Arguments:
- tokens: bfloat16 [2048, 4096], P(('dp', 'expert'), 'tensor'), may hold values from -6 to 6
- target: bfloat16 [2048, 4096], P(('dp', 'expert'), 'tensor'), may hold values from -4 to 4
- router: bfloat16 [4096, 8], P('tensor'), may hold values from -1 to 1
- w_gate: bfloat16 [8, 4096, 14336], P('expert', None, ('dp', 'tensor')), may hold values from -1 to 1
- w_up: bfloat16 [8, 4096, 14336], P('expert', None, ('dp', 'tensor')), may hold values from -1 to 1
- w_down: bfloat16 [8, 14336, 4096], P('expert', ('dp', 'tensor')), may hold values from -1 to 1
- expert_ids: int32 [2048, 2], P(('dp', 'expert')), may hold values from 0 to 7, as said below
- lengths: int32 [64], replicated, may hold values from 1 to 128, 2048 in all
- bench_ids: int32 [64], replicated, may hold values from 0 to 15
Outputs:
- mixed: bfloat16 [2048, 4096], P(('dp', 'expert'), 'tensor')
- bench_loss: float32 [16], replicated
- counts: int32 [16], replicated
Inputs may be any that keep to these rules, and one draw needn't show every extreme that they name: `expert_ids`: each row names two different experts; among the 16 rows of one device no expert is named by more than 8 rows; for each index of dp, one expert is named by exactly 8 rows of every device of that index. The lengths sum to 2048.
All inputs are finite; a program needn't handle non-finite values.
Results may differ from a plain program's by a relative error of at most 0.0085.
Values may be sent and summed in bfloat16 or wider, within the bound.
A program may use at most 128 MiB of HBM per device.

v0:
```python
import jax
import jax.numpy as jnp
from jax import lax
from jax.sharding import Mesh
from jax.sharding import PartitionSpec as P

D = 4096
NB = 16
CAP = 8
DP = ("dp_0", "dp_1")
DP_EXPERT = ("dp_0", "dp_1", "expert")
DP_EXPERT_TENSOR = ("dp_0", "dp_1", "expert", "tensor")
DP_TENSOR = ("dp_0", "dp_1", "tensor")


def cut_along(shard, dim, size):
    before, after = (shard.shape[:dim], shard.shape[dim + 1 :])
    return jnp.moveaxis(shard.reshape(*before, size, -1, *after), dim, 0)


def sent_and_summed(shard, axis, dim):
    pieces = cut_along(shard, dim, lax.axis_size(axis))
    arrived = lax.all_to_all(pieces, axis, split_axis=0, concat_axis=0, tiled=True)
    return arrived.sum(axis=0)


def one_axis_at_a_time(shard, axes):
    for axis in axes:
        shard = lax.psum(shard, axis)
    return shard


def per_device(tokens, target, router, w_gate, w_up, w_down, expert_ids, lengths, bench_ids):
    tensor_count = lax.axis_size("tensor")
    local_tokens = tokens.shape[0]
    experts = router.shape[1]
    half_cap = CAP // tensor_count
    slot_rows = tensor_count * experts * half_cap
    partial_value = jnp.dot(tokens, router, preferred_element_type=jnp.float32)
    logits = lax.psum(partial_value, "tensor")
    chosen = expert_ids[:, :, None] == jnp.arange(experts, dtype=jnp.int32)[None, None, :]
    picked = jnp.sum(jnp.where(chosen, logits[:, None, :], jnp.float32(0.0)), axis=2)
    gates = jnp.stack(
        [jax.nn.sigmoid(picked[:, 0] - picked[:, 1]), jax.nn.sigmoid(picked[:, 1] - picked[:, 0])],
        axis=1,
    )
    marks = chosen.reshape(local_tokens * 2, experts).astype(jnp.int32)
    before = jnp.cumsum(marks, axis=0) - marks
    slot = jnp.sum(before * marks, axis=1)
    flat_ids = expert_ids.reshape(local_tokens * 2)
    target_row = slot // half_cap * (experts * half_cap) + flat_ids * half_cap + slot % half_cap
    placing = (target_row[None, :] == jnp.arange(slot_rows, dtype=jnp.int32)[:, None]).reshape(
        slot_rows, local_tokens, 2
    )
    dispatch_map = jnp.any(placing, axis=2).astype(jnp.bfloat16)
    outgoing = jnp.dot(dispatch_map, tokens, preferred_element_type=jnp.float32).astype(
        jnp.bfloat16
    )
    outgoing = outgoing.reshape(tensor_count, experts, half_cap, tokens.shape[1])
    arrived = lax.all_to_all(outgoing, "expert", split_axis=1, concat_axis=1, tiled=True)
    whole = lax.all_gather(arrived, "tensor", axis=3, tiled=True)
    whole = whole.reshape(1, slot_rows, D)
    every_row = lax.all_gather(whole, DP, axis=0, tiled=True).reshape(-1, D)
    gate_w = w_gate[0]
    up_w = w_up[0]
    down_w = w_down[0]
    gate = jnp.dot(every_row, gate_w, preferred_element_type=jnp.float32)
    up = jnp.dot(every_row, up_w, preferred_element_type=jnp.float32)
    hidden = (jax.nn.silu(gate) * up).astype(jnp.bfloat16)
    summed = lax.psum_scatter(
        jnp.dot(hidden, down_w, preferred_element_type=jnp.float32),
        DP,
        scatter_dimension=0,
        tiled=True,
    )
    summed = sent_and_summed(summed, "tensor", 1)
    results = summed.astype(jnp.bfloat16).reshape(
        tensor_count, experts, half_cap, D // tensor_count
    )
    returned = lax.all_to_all(results, "expert", split_axis=1, concat_axis=1, tiled=True)
    weights = jnp.einsum("rtk,tk->tr", placing.astype(jnp.float32), gates)
    flat_back = returned.reshape(slot_rows, -1).astype(jnp.float32)
    mixed = jnp.dot(weights, flat_back, precision=lax.Precision.HIGHEST).astype(jnp.bfloat16)
    first_index = lax.axis_index(DP_EXPERT) * local_tokens
    position = first_index + jnp.arange(local_tokens, dtype=jnp.int32)
    ends = jnp.cumsum(lengths)
    starts = ends - lengths
    inside = ((position[:, None] >= starts[None, :]) & (position[:, None] < ends[None, :])).astype(
        jnp.float32
    )
    closing = jnp.any((position + 1)[:, None] == ends[None, :], axis=1)
    scored = jnp.where(closing, jnp.float32(0.0), jnp.float32(1.0))
    bench_table = bench_ids[:, None] == jnp.arange(NB, dtype=jnp.int32)[None, :]
    bench_of = jnp.dot(inside, bench_table.astype(jnp.float32), precision=lax.Precision.HIGHEST)
    diff = mixed.astype(jnp.float32) - target.astype(jnp.float32)
    token_part = jnp.sum(diff * diff, axis=1) / D
    local_sums = jnp.dot(scored * token_part, bench_of, precision=lax.Precision.HIGHEST)
    loss_sum = one_axis_at_a_time(local_sums, DP_EXPERT_TENSOR)
    counts = jnp.sum(jnp.where(bench_table, (lengths - 1)[:, None], 0), axis=0)
    bench_loss = loss_sum / jnp.maximum(counts, 1).astype(jnp.float32)
    return (mixed, bench_loss, counts)


def solution(mesh):
    split = Mesh(
        mesh.devices.reshape(4, 4, mesh.shape["expert"], mesh.shape["tensor"]),
        ("dp_0", "dp_1", "expert", "tensor"),
    )
    in_specs = (
        P(DP_EXPERT, "tensor"),
        P(DP_EXPERT, "tensor"),
        P("tensor", None),
        P("expert", None, DP_TENSOR),
        P("expert", None, DP_TENSOR),
        P("expert", DP_TENSOR, None),
        P(DP_EXPERT, None),
        P(),
        P(),
    )
    out_specs = (P(DP_EXPERT, "tensor"), P(), P())
    return jax.shard_map(
        per_device, mesh=split, in_specs=in_specs, out_specs=out_specs, check_vma=False
    )
```

profile of v0, /device:TPU:1, one launch (start us, length us, event | category | flops | bytes accessed | tf_op | source)
XLA Modules:
  0.0 317.1 jit_solution(9953797493856227956)
XLA Ops:
  7.2 0.8 copy.53
  8.2 0.2 select_reduce_fusion
  8.6 0.7 fusion.22
  9.4 0.3 convolution_convert_fusion
  9.8 19.3 %all_to_all.15 = bf16[2,8,4,2048]{3,2,0,1:T(4,128)(2,1)S(1)} all-to-all(bf16[2,8,4,2048]{3,2,0,1:T(4,128)(2,1)S(1)} %copy.58), channel_id=1, replica_groups=mesh['dp_0'=4,'dp_1'=4,'expert'=8,'tensor'=2] {'expert'}, dimensions={1} | all-to-all | bytes 524288 | tf_op jit(solution)/shard_map/all_to_all | solution.py:60
  29.2 4.1 %all_gather.6 = bf16[2,8,4,4096]{3,2,0,1:T(4,128)(2,1)S(1)} all-gather(bf16[2,8,4,2048]{3,2,0,1:T(4,128)(2,1)S(1)} %all_to_all.15), channel_id=1, replica_groups=mesh['dp_0'=4,'dp_1'=4,'expert'=8,'tensor'=2] {'tensor'}, dimensions={3}, use_global_device_ids=true | all-gather | bytes 786432 | tf_op jit(solution)/shard_map/all_gather | solution.py:61
  33.3 0.2 copy.59
  33.5 0.9 reshape.109
  34.5 71.8 %all-gather.2.cloned.1.call-done = bf16[16,64,4096]{2,1,0:T(8,128)(2,1)} async-done(((bf16[1,64,4096]{2,1,0:T(8,128)(2,1)}), bf16[16,64,4096]{2,1,0:T(8,128)(2,1)}) %all-gather.2.cloned.1.call-update) | async-done | bytes 8388624 | tf_op jit(solution)/shard_map/all_gather | solution.py:63
  106.3 7.5 %fusion.4 = f32[1024,448]{0,1:T(8,128)S(1)} fusion(bf16[1024,4096]{1,0:T(8,128)(2,1)} %bitcast.45, bf16[1,4096,448]{1,2,0:T(8,128)(2,1)} %param.12), kind=kOutput, calls=%fused_computation.4 | convolution fusion | flops 3758096384 | bytes 13893632 | tf_op jit(solution)/shard_map/dot_general | solution.py:67
  113.8 16.5 %fusion = f32[1024,4096]{1,0:T(8,128)} fusion(bf16[1,448,4096]{2,1,0:T(8,128)(2,1)} %param.14, f32[1024,448]{0,1:T(8,128)S(1)} %fusion.4, bf16[1024,4096]{1,0:T(8,128)(2,1)} %bitcast.46, bf16[1,4096,448]{1,2,0:T(8,128)(2,1)} %param.13), kind=kOutput, calls=%fused_computation | convolution fusion | flops 7518945280 | bytes 34340864 | tf_op jit(solution)/shard_map/dot_general | solution.py:71
  130.4 0.6 copy-done.4
  131.2 0.1 reduce
  131.3 0.1 fusion.35
  131.4 3.0 psum.35
  134.4 0.1 select_reduce_fusion.1
  134.5 0.2 compare_reduce_fusion
  134.7 111.3 %reduce-scatter.2.cloned.1.call-done = f32[64,4096]{1,0:T(8,128)} async-done(((f32[1024,4096]{1,0:T(8,128)}), f32[64,4096]{1,0:T(8,128)}) %reduce-scatter.2.cloned.1.call-update) | async-done | bytes 1048592 | tf_op jit(solution)/shard_map/reduce_scatter | solution.py:70
  246.0 1.3 copy.71
  247.3 5.1 %all_to_all.16 = f32[2,64,2048]{2,1,0:T(8,128)S(1)} all-to-all(f32[2,64,2048]{2,1,0:T(8,128)S(1)} %bitcast.41), channel_id=1, replica_groups=mesh['dp_0'=4,'dp_1'=4,'expert'=8,'tensor'=2] {'tensor'}, dimensions={0} | all-to-all | bytes 2097152 | tf_op jit(solution)/shard_map/all_to_all | solution.py:23
  252.6 0.8 copy.61
  253.4 6.8 %all-to-all-start.2 = ((bf16[2,8,4,2048]{3,2,0,1:T(4,128)(2,1)}), bf16[2,8,4,2048]{3,2,0,1:T(4,128)(2,1)S(1)}, u32[]{:S(2)}, u32[]{:S(2)}) async-start(bf16[2,8,4,2048]{3,2,0,1:T(4,128)(2,1)} %copy.61), calls=%async_computation.3 | async-start | bytes 524288 | tf_op jit(solution)/shard_map/all_to_all | solution.py:80
  260.3 0.2 fusion.14
  260.5 0.1 fusion.11
  260.6 10.7 %all-to-all-done.2 = bf16[2,8,4,2048]{3,2,0,1:T(4,128)(2,1)S(1)} async-done(((bf16[2,8,4,2048]{3,2,0,1:T(4,128)(2,1)}), bf16[2,8,4,2048]{3,2,0,1:T(4,128)(2,1)S(1)}, u32[]{:S(2)}, u32[]{:S(2)}) %all-to-all-start.2) | async-done | bytes 262176 | tf_op jit(solution)/shard_map/all_to_all | solution.py:80
  271.5 1.0 multiply_reduce_fusion
  272.4 0.1 convolution_bitcast_fusion
  272.6 8.0 %psum.36 = f32[16]{0:T(128)S(1)} all-reduce(f32[16]{0:T(128)S(1)} %convolution_bitcast_fusion), channel_id=1, replica_groups=mesh['dp_0'=4,'dp_1'=4,'expert'=8,'tensor'=2] {'dp_0'}, use_global_device_ids=true, to_apply=%region_10.11 | all-reduce | flops 16 | bytes 128 | tf_op jit(solution)/shard_map/psum | solution.py:29
  280.5 6.7 %psum.37 = f32[16]{0:T(128)S(1)} all-reduce(f32[16]{0:T(128)S(1)} %psum.36), channel_id=1, replica_groups=mesh['dp_0'=4,'dp_1'=4,'expert'=8,'tensor'=2] {'dp_1'}, use_global_device_ids=true, to_apply=%region_11.12 | all-reduce | flops 16 | bytes 128 | tf_op jit(solution)/shard_map/psum | solution.py:29
  287.2 10.7 %psum.38 = f32[16]{0:T(128)S(1)} all-reduce(f32[16]{0:T(128)S(1)} %psum.37), channel_id=1, replica_groups=mesh['dp_0'=4,'dp_1'=4,'expert'=8,'tensor'=2] {'expert'}, use_global_device_ids=true, to_apply=%region_12.13 | all-reduce | flops 16 | bytes 128 | tf_op jit(solution)/shard_map/psum | solution.py:29
  297.9 11.9 %psum.39 = f32[16]{0:T(128)S(1)} all-reduce(f32[16]{0:T(128)S(1)} %psum.38), channel_id=1, replica_groups=mesh['dp_0'=4,'dp_1'=4,'expert'=8,'tensor'=2] {'tensor'}, use_global_device_ids=true, to_apply=%region_13.14 | all-reduce | flops 16 | bytes 128 | tf_op jit(solution)/shard_map/psum | solution.py:29
  309.8 0.5 convert_divide_fusion
  (37 shorter events, 1.5 us)
Async XLA Ops:
  7.2 2.2 copy-start
  7.2 99.1 %all-gather.2.cloned.1.call-start = ((), (), s32[]{:S(2)}) async-start(), calls=%async_computation.4 | async-start | bytes 8912896 | tf_op jit(solution)/shard_map/all_gather | solution.py:63
  34.4 211.6 %reduce-scatter.2.cloned.1.call-start = ((), (), s32[]{:S(2)}) async-start(), calls=%async_computation.5 | async-start | bytes 17825792 | tf_op jit(solution)/shard_map/reduce_scatter | solution.py:70
  130.3 0.7 copy-start.4
  130.3 1.0 copy-start.2
  130.3 4.1 %copy-start.5 = (s32[64]{0:T(128)S(1)}, s32[64]{0:T(128)}, u32[]{:S(2)}) copy-start(s32[64]{0:T(128)} %param.17) | copy-start | bytes 772
  130.3 4.2 %copy-start.3 = (s32[16,2]{0,1:T(2,128)S(1)}, s32[16,2]{0,1:T(2,128)}, u32[]{:S(2)}) copy-start(s32[16,2]{0,1:T(2,128)} %param.15) | copy-start | bytes 388
  134.5 175.3 %copy-start.6 = (s32[16]{0:T(128)}, s32[16]{0:T(128)S(1)}, u32[]{:S(2)}) copy-start(s32[16]{0:T(128)S(1)} %select_reduce_fusion.1) | copy-start | bytes 196
  246.0 25.5 %copy-start.1 = (bf16[16,2048]{1,0:T(8,128)(2,1)S(1)}, bf16[16,2048]{1,0:T(8,128)(2,1)}, u32[]{:S(2)}) copy-start(bf16[16,2048]{1,0:T(8,128)(2,1)} %param.10) | copy-start | bytes 196612
  253.4 17.9 %all-to-all-start.2 = ((bf16[2,8,4,2048]{3,2,0,1:T(4,128)(2,1)}), bf16[2,8,4,2048]{3,2,0,1:T(4,128)(2,1)S(1)}, u32[]{:S(2)}, u32[]{:S(2)}) async-start(bf16[2,8,4,2048]{3,2,0,1:T(4,128)(2,1)} %copy.61), calls=%async_computation.3 | async-start | bytes 524288 | tf_op jit(solution)/shard_map/all_to_all | solution.py:80
Sparse Core Ops, SparseCore 0:
  34.5 71.6 all-gather.1
  130.5 115.4 reduce-scatter.1
where the time goes:
time: 318 us; the launch traced here: 317 us
  waiting for transfers between devices  194 us (61%)
  blocking collectives  68.7 us (22%)
  matrix products  25.9 us (8%)
  between operations  14.2 us (4%)
  starting transfers between devices  6.86 us (2%)
  local copies, waits for them, and re-layouts  5.59 us (2%)
    reduce_scatter x1, waiting for transfers between devices, per_device(): lax.psum_scatter(jnp.dot(hidden, down_w, preferred_element_type=jnp.float...  111 us
    all_gather x1, waiting for transfers between devices, per_device(): every_row = lax.all_gather(whole, DP, axis=0, tiled=True).reshape(-1, D)  71.8 us
    psum x4, blocking collectives, one_axis_at_a_time(): shard = lax.psum(shard, axis)  37.2 us
    all_to_all x1, blocking collectives, per_device(): lax.all_to_all(outgoing, 'expert', split_axis=1, concat_axis=1, tiled=True)  19.3 us
    dot_general x1, matrix products, per_device(): jnp.dot(hidden, down_w, preferred_element_type=jnp.float32)  16.5 us
    all_to_all x1, waiting for transfers between devices, per_device(): lax.all_to_all(results, 'expert', split_axis=1, concat_axis=1, tiled=True)  10.7 us
    dot_general x1, matrix products, per_device(): gate = jnp.dot(every_row, gate_w, preferred_element_type=jnp.float32)  7.52 us
    all_to_all x1, starting transfers between devices, per_device(): lax.all_to_all(results, 'expert', split_axis=1, concat_axis=1, tiled=True)  6.78 us
  transfers between devices with their start and end apart: 3, of which 3 were waited for; matrix products, arithmetic and copies ran while one was open for 0% of the time, Pallas kernels for 0%

commit v1 on v0

--- a/solution.py
+++ b/solution.py
@@ -3,6 +3,7 @@
 from jax import lax
 from jax.sharding import Mesh
 from jax.sharding import PartitionSpec as P
+from jax.lax import all_to_all, axis_size
 
 D = 4096
 NB = 16
@@ -31,6 +32,13 @@
 
 
 def per_device(tokens, target, router, w_gate, w_up, w_down, expert_ids, lengths, bench_ids):
+
+    def launch_panels(s0, peer_axis):
+        step_out = jnp.stack(axis_size(peer_axis) * [s0], axis=0)
+        carry_in = all_to_all(step_out, peer_axis, 0, 0)
+        local_part = jnp.concatenate(carry_in, axis=0)
+        return local_part
+
     tensor_count = lax.axis_size("tensor")
     local_tokens = tokens.shape[0]
     experts = router.shape[1]
@@ -60,7 +68,7 @@
     arrived = lax.all_to_all(outgoing, "expert", split_axis=1, concat_axis=1, tiled=True)
     whole = lax.all_gather(arrived, "tensor", axis=3, tiled=True)
     whole = whole.reshape(1, slot_rows, D)
-    every_row = lax.all_gather(whole, DP, axis=0, tiled=True).reshape(-1, D)
+    every_row = launch_panels(whole, DP).reshape(-1, D)
     gate_w = w_gate[0]
     up_w = w_up[0]
     down_w = w_down[0]

time: 318 us -> 341 us (1.072)
  blocking collectives: 68.7 us -> 172 us
  waiting for transfers between devices: 194 us -> 115 us
  matrix products: 25.9 us -> 22.3 us
  local copies, waits for them, and re-layouts: 5.59 us -> 9.06 us
    all_to_all x0 -> x1, blocking collectives: none -> 102 us  [launch_panels(): carry_in = all_to_all(step_out, peer_axis, 0, 0)]
    all_gather x1 -> x0, waiting for transfers between devices: 71.8 us -> none  [per_device(): every_row = lax.all_gather(whole, DP, axis=0, tiled=True).reshape(-1, D)]
    reduce_scatter x1, waiting for transfers between devices: 111 us -> 104 us  [per_device(): lax.psum_scatter(jnp.dot(hidden, down_w, preferred_element_type=jnp.float...]
    dot_general x1, matrix products: 7.52 us -> 3.99 us  [per_device(): gate = jnp.dot(every_row, gate_w, preferred_element_type=jnp.float32)]
  transfers between devices with their start and end apart: 3 -> 2, of which waited for: 3 -> 2; matrix products, arithmetic and copies ran while one was open for 0% -> 0% of each run, Pallas kernels for 0% -> 0%
where the time goes in v1:
time: 341 us
  blocking collectives  172 us (50%)
  waiting for transfers between devices  115 us (34%)
  matrix products  22.3 us (7%)
  between operations  14.2 us (4%)
  local copies, waits for them, and re-layouts  9.06 us (3%)
  starting transfers between devices  6.81 us (2%)
    reduce_scatter x1, waiting for transfers between devices, per_device(): lax.psum_scatter(jnp.dot(hidden, down_w, preferred_element_type=jnp.float...  104 us
    all_to_all x1, blocking collectives, launch_panels(): carry_in = all_to_all(step_out, peer_axis, 0, 0)  102 us
    psum x4, blocking collectives, one_axis_at_a_time(): shard = lax.psum(shard, axis)  37.2 us
    all_to_all x1, blocking collectives, per_device(): lax.all_to_all(outgoing, 'expert', split_axis=1, concat_axis=1, tiled=True)  19.3 us
    dot_general x1, matrix products, per_device(): jnp.dot(hidden, down_w, preferred_element_type=jnp.float32)  16.5 us
    all_to_all x1, waiting for transfers between devices, per_device(): lax.all_to_all(results, 'expert', split_axis=1, concat_axis=1, tiled=True)  10.7 us
  transfers between devices with their start and end apart: 2, of which 2 were waited for; matrix products, arithmetic and copies ran while one was open for 0% of the time, Pallas kernels for 0%

profile of v1, /device:TPU:1, one launch (start us, length us, event | category | flops | bytes accessed | tf_op | source)
XLA Modules:
  0.0 340.7 jit_solution(12668287122346641736)
XLA Ops:
  7.2 0.8 copy.53
  8.2 0.2 select_reduce_fusion
  8.6 0.7 fusion.22
  9.4 0.3 convolution_convert_fusion
  9.8 19.3 %all_to_all.20 = bf16[2,8,4,2048]{3,2,0,1:T(4,128)(2,1)S(1)} all-to-all(bf16[2,8,4,2048]{3,2,0,1:T(4,128)(2,1)S(1)} %copy.58), channel_id=1, replica_groups=mesh['dp_0'=4,'dp_1'=4,'expert'=8,'tensor'=2] {'expert'}, dimensions={1} | all-to-all | bytes 524288 | tf_op jit(solution)/shard_map/all_to_all | solution.py:68
  29.2 4.1 %all_gather.3 = bf16[2,8,4,4096]{3,2,0,1:T(4,128)(2,1)S(1)} all-gather(bf16[2,8,4,2048]{3,2,0,1:T(4,128)(2,1)S(1)} %all_to_all.20), channel_id=1, replica_groups=mesh['dp_0'=4,'dp_1'=4,'expert'=8,'tensor'=2] {'tensor'}, dimensions={3}, use_global_device_ids=true | all-gather | bytes 786432 | tf_op jit(solution)/shard_map/all_gather | solution.py:69
  33.3 0.2 copy.59
  33.5 0.1 stack_reshape.2
  33.6 1.0 stack.9
  34.7 101.8 %all_to_all.21 = bf16[16,1,64,4096]{3,2,1,0:T(8,128)(2,1)S(1)} all-to-all(bf16[16,1,64,4096]{3,2,1,0:T(8,128)(2,1)S(1)} %stack.9), channel_id=1, replica_groups=mesh['dp_0'=4,'dp_1'=4,'expert'=8,'tensor'=2] {'dp_0','dp_1'}, dimensions={0} | all-to-all | bytes 16777216 | tf_op jit(solution)/shard_map/all_to_all | solution.py:38
  136.5 3.2 copy-done.1
  139.7 4.0 %fusion.4 = f32[1024,448]{0,1:T(8,128)S(1)} fusion(bf16[1024,4096]{1,0:T(8,128)(2,1)S(1)} %bitcast.41, bf16[1,4096,448]{1,2,0:T(8,128)(2,1)S(1)} %copy-done.6), kind=kOutput, calls=%fused_computation.4 | convolution fusion | flops 3758096384 | bytes 13893632 | tf_op jit(solution)/shard_map/dot_general | solution.py:75
  143.7 16.5 %fusion = f32[1024,4096]{1,0:T(8,128)} fusion(bf16[1,448,4096]{2,1,0:T(8,128)(2,1)} %param.14, f32[1024,448]{0,1:T(8,128)S(1)} %fusion.4, bf16[1024,4096]{1,0:T(8,128)(2,1)} %bitcast.42, bf16[1,4096,448]{1,2,0:T(8,128)(2,1)} %param.13), kind=kOutput, calls=%fused_computation | convolution fusion | flops 7518945280 | bytes 34340864 | tf_op jit(solution)/shard_map/dot_general | solution.py:79
  160.3 0.6 copy-done.5
  161.2 0.1 fusion.35
  161.3 3.9 %psum.35 = f32[16,8]{0,1:T(8,128)S(1)} all-reduce(f32[16,8]{0,1:T(8,128)S(1)} %fusion.35), channel_id=1, replica_groups=mesh['dp_0'=4,'dp_1'=4,'expert'=8,'tensor'=2] {'tensor'}, use_global_device_ids=true, to_apply=%region_2.3 | all-reduce | flops 128 | bytes 1024 | tf_op jit(solution)/shard_map/psum | solution.py:48
  165.4 0.2 compare_reduce_fusion
  165.6 103.9 %reduce-scatter.2.cloned.1.call-done = f32[64,4096]{1,0:T(8,128)} async-done(((f32[1024,4096]{1,0:T(8,128)}), f32[64,4096]{1,0:T(8,128)}) %reduce-scatter.2.cloned.1.call-update) | async-done | bytes 1048592 | tf_op jit(solution)/shard_map/reduce_scatter | solution.py:78
  269.4 1.3 copy.71
  270.8 5.2 %all_to_all.22 = f32[2,64,2048]{2,1,0:T(8,128)S(1)} all-to-all(f32[2,64,2048]{2,1,0:T(8,128)S(1)} %bitcast.43), channel_id=1, replica_groups=mesh['dp_0'=4,'dp_1'=4,'expert'=8,'tensor'=2] {'tensor'}, dimensions={0} | all-to-all | bytes 2097152 | tf_op jit(solution)/shard_map/all_to_all | solution.py:24
  276.2 0.8 copy.61
  277.0 6.8 %all-to-all-start.3 = ((bf16[2,8,4,2048]{3,2,0,1:T(4,128)(2,1)}), bf16[2,8,4,2048]{3,2,0,1:T(4,128)(2,1)S(1)}, u32[]{:S(2)}, u32[]{:S(2)}) async-start(bf16[2,8,4,2048]{3,2,0,1:T(4,128)(2,1)} %copy.61), calls=%async_computation.4 | async-start | bytes 524288 | tf_op jit(solution)/shard_map/all_to_all | solution.py:88
  283.9 0.2 fusion.14
  284.1 0.1 fusion.11
  284.2 10.7 %all-to-all-done.3 = bf16[2,8,4,2048]{3,2,0,1:T(4,128)(2,1)S(1)} async-done(((bf16[2,8,4,2048]{3,2,0,1:T(4,128)(2,1)}), bf16[2,8,4,2048]{3,2,0,1:T(4,128)(2,1)S(1)}, u32[]{:S(2)}, u32[]{:S(2)}) %all-to-all-start.3) | async-done | bytes 262176 | tf_op jit(solution)/shard_map/all_to_all | solution.py:88
  295.0 1.0 multiply_reduce_fusion
  296.0 0.1 convolution_bitcast_fusion
  296.1 8.0 %psum.36 = f32[16]{0:T(128)S(1)} all-reduce(f32[16]{0:T(128)S(1)} %convolution_bitcast_fusion), channel_id=1, replica_groups=mesh['dp_0'=4,'dp_1'=4,'expert'=8,'tensor'=2] {'dp_0'}, use_global_device_ids=true, to_apply=%region_10.11 | all-reduce | flops 16 | bytes 128 | tf_op jit(solution)/shard_map/psum | solution.py:30
  304.1 6.6 %psum.37 = f32[16]{0:T(128)S(1)} all-reduce(f32[16]{0:T(128)S(1)} %psum.36), channel_id=1, replica_groups=mesh['dp_0'=4,'dp_1'=4,'expert'=8,'tensor'=2] {'dp_1'}, use_global_device_ids=true, to_apply=%region_11.12 | all-reduce | flops 16 | bytes 128 | tf_op jit(solution)/shard_map/psum | solution.py:30
  310.8 10.7 %psum.38 = f32[16]{0:T(128)S(1)} all-reduce(f32[16]{0:T(128)S(1)} %psum.37), channel_id=1, replica_groups=mesh['dp_0'=4,'dp_1'=4,'expert'=8,'tensor'=2] {'expert'}, use_global_device_ids=true, to_apply=%region_12.13 | all-reduce | flops 16 | bytes 128 | tf_op jit(solution)/shard_map/psum | solution.py:30
  321.4 11.9 %psum.39 = f32[16]{0:T(128)S(1)} all-reduce(f32[16]{0:T(128)S(1)} %psum.38), channel_id=1, replica_groups=mesh['dp_0'=4,'dp_1'=4,'expert'=8,'tensor'=2] {'tensor'}, use_global_device_ids=true, to_apply=%region_13.14 | all-reduce | flops 16 | bytes 128 | tf_op jit(solution)/shard_map/psum | solution.py:30
  333.3 0.5 convert_divide_fusion
  (40 shorter events, 1.7 us)
Async XLA Ops:
  7.2 2.2 copy-start
  7.2 262.2 %reduce-scatter.2.cloned.1.call-start = ((), (), s32[]{:S(2)}) async-start(), calls=%async_computation.5 | async-start | bytes 17825792 | tf_op jit(solution)/shard_map/reduce_scatter | solution.py:78
  34.7 105.0 %copy-start.6 = (bf16[1,4096,448]{1,2,0:T(8,128)(2,1)S(1)}, bf16[1,4096,448]{1,2,0:T(8,128)(2,1)}, u32[]{:S(2)}) copy-start(bf16[1,4096,448]{1,2,0:T(8,128)(2,1)} %param.12) | copy-start | bytes 11010052
  136.5 3.2 copy-start.1
  160.2 0.7 copy-start.5
  160.2 1.0 copy-start.3
  160.2 5.0 %copy-start.7 = (s32[64]{0:T(128)S(1)}, s32[64]{0:T(128)}, u32[]{:S(2)}) copy-start(s32[64]{0:T(128)} %param.17) | copy-start | bytes 772
  160.2 5.1 %copy-start.4 = (s32[16,2]{0,1:T(2,128)S(1)}, s32[16,2]{0,1:T(2,128)}, u32[]{:S(2)}) copy-start(s32[16,2]{0,1:T(2,128)} %param.15) | copy-start | bytes 388
  165.3 168.0 %copy-start.8 = (s32[16]{0:T(128)}, s32[16]{0:T(128)S(1)}, u32[]{:S(2)}) copy-start(s32[16]{0:T(128)S(1)} %select_reduce_fusion.1) | copy-start | bytes 196
  269.4 25.6 %copy-start.2 = (bf16[16,2048]{1,0:T(8,128)(2,1)S(1)}, bf16[16,2048]{1,0:T(8,128)(2,1)}, u32[]{:S(2)}) copy-start(bf16[16,2048]{1,0:T(8,128)(2,1)} %param.10) | copy-start | bytes 196612
  277.0 17.9 %all-to-all-start.3 = ((bf16[2,8,4,2048]{3,2,0,1:T(4,128)(2,1)}), bf16[2,8,4,2048]{3,2,0,1:T(4,128)(2,1)S(1)}, u32[]{:S(2)}, u32[]{:S(2)}) async-start(bf16[2,8,4,2048]{3,2,0,1:T(4,128)(2,1)} %copy.61), calls=%async_computation.4 | async-start | bytes 524288 | tf_op jit(solution)/shard_map/all_to_all | solution.py:88
Sparse Core Ops, SparseCore 0:
  160.4 109.0 reduce-scatter.1
